TPU v7x, 256 devices: a whole 4x4x8 slice. The times are simulated.
256 devices in a mesh: grp: 32 (over y, z), row: 8 (over x, core).
Axes of the slice: x: 4, y: 4, z: 8, core: 2. Of those that a mesh axis runs over, the one named last changes fastest.
Arguments:
- block: bfloat16 [65536, 1024], P(('grp', 'row')), may hold values from -6 to 6
- degree: int32 [65536], P(('grp', 'row')), may hold values from 1 to 3
- tile_values: bfloat16 [16384, 128, 128], P(('grp', 'row')), may hold values from -0.1875 to 0.1875
- tile_rows: int32 [16384], P(('grp', 'row')), may hold values from 0 to 1
- tile_cols: int32 [16384], P(('grp', 'row')), may hold values from 0 to 47
- tile_count: int32 [256], P(('grp', 'row')), may hold values from 24 to 64, as said below
- send_tiles: int32 [256, 32], P(('grp', 'row')), may hold values from 0 to 1
Outputs:
- logs: bfloat16 [65536, 1024], P(('grp', 'row'))
- gram: float32 [32768, 1024], P(('grp', 'row'))
Inputs may be any that keep to these rules, and one draw needn't show every extreme that they name: Slots of a device at positions tile_count or later are padding; some device has all 64 slots live.
All inputs are finite; a program needn't handle non-finite values.
Results may differ from a plain program's by a relative error of at most 0.014.
Values may be sent and summed in bfloat16 or wider, within the bound.
A program may use at most 128 MiB of HBM per device.

v0:
```python
import jax
import jax.numpy as jnp
from jax import lax
from jax.sharding import PartitionSpec as P

POWERS = 2


def tile_products(sources, tile_values, tile_rows, tile_cols, live_count, row_tiles):
    slots = tile_values.shape[0]
    tile = tile_values.shape[1]
    width = sources.shape[2]
    block_size = 8
    tile_ids = jnp.arange(row_tiles, dtype=jnp.int32)

    def add_block(block_index, totals):
        first_slot = block_index * block_size
        values_block = lax.dynamic_slice_in_dim(tile_values, first_slot, block_size, 0)
        column_ids = lax.dynamic_slice_in_dim(tile_cols, first_slot, block_size, 0)
        row_ids = lax.dynamic_slice_in_dim(tile_rows, first_slot, block_size, 0)
        picked = jnp.take(sources, column_ids, axis=0)
        products = jnp.einsum(
            "sik,skf->sif", values_block, picked, preferred_element_type=jnp.float32
        )
        live_mask = first_slot + jnp.arange(block_size, dtype=jnp.int32) < live_count
        weights = ((row_ids[None, :] == tile_ids[:, None]) & live_mask[None, :]).astype(jnp.float32)
        return totals + jnp.einsum("rs,sif->rif", weights, products)

    start_totals = jnp.zeros((row_tiles, tile, width), jnp.float32)
    return lax.fori_loop(0, slots // block_size, add_block, start_totals)


def body(block, degree, tile_values, tile_rows, tile_cols, tile_count, send_tiles):
    rows_here, width = block.shape
    tile = tile_values.shape[1]
    row_tiles = rows_here // tile
    ranks = lax.axis_size("row")
    divisor = degree.astype(jnp.float32)[:, None]
    current = block
    power_sum = jnp.zeros(block.shape, jnp.float32)
    for power in range(POWERS):
        gathered = lax.all_gather(current, "row", axis=0, tiled=True)
        own_tiles = current.reshape(row_tiles, tile, width)
        outgoing = jnp.take(own_tiles, send_tiles[0], axis=0)
        incoming = lax.all_to_all(outgoing, "grp", split_axis=0, concat_axis=0, tiled=True)
        sources = jnp.concatenate([gathered.reshape(-1, tile, width), incoming], axis=0)
        summed = tile_products(sources, tile_values, tile_rows, tile_cols, tile_count[0], row_tiles)
        current = (summed.reshape(rows_here, width) / divisor).astype(jnp.bfloat16)
        power_sum = power_sum + current.astype(jnp.float32)
    logs = jnp.log(jnp.maximum(3.0 * power_sum, 1.0)).astype(jnp.bfloat16)
    share = width // ranks
    contract = (((0,), (0,)), ((), ()))
    everyone = lax.all_gather(logs, "row", axis=0, tiled=True)
    columns = lax.dynamic_slice_in_dim(everyone, lax.axis_index("row") * share, share, 1)
    gram = lax.dot_general(columns, everyone, contract, preferred_element_type=jnp.float32)
    return (logs, gram / (rows_here * ranks))


def solution(mesh):
    placed = (
        P(("grp", "row"), None),
        P(("grp", "row")),
        P(("grp", "row"), None, None),
        P(("grp", "row")),
        P(("grp", "row")),
        P(("grp", "row")),
        P(("grp", "row"), None),
    )
    return jax.shard_map(
        body,
        mesh=mesh,
        in_specs=placed,
        out_specs=(P(("grp", "row"), None), P(("grp", "row"), None)),
        check_vma=False,
    )
```

profile of v0, /device:TPU:1, one launch (start us, length us, event | category | flops | bytes accessed | tf_op | source)
XLA Modules:
  0.0 729.4 jit_solution(15432242028121098063)
XLA Ops:
  8.5 5.9 gather_fusion.2
  14.4 7.5 %broadcast_select_fusion.1 = bf16[32,128,1024]{2,1,0:T(8,128)(2,1)} fusion(bf16[32,128,1024]{2,1,0:T(8,128)(2,1)} %gather_fusion.2, pred[32]{0:T(512)(128)(4,1)S(1)} %compare_and_fusion.2), kind=kLoop, calls=%fused_computation.49 | loop fusion | flops 4194304 | bytes 16777248 | tf_op jit(solution)/shard_map/jit(_take)/select_n | solution.py:44
  21.9 12.3 %all-to-all-start = ((bf16[32,128,1024]{2,1,0:T(8,128)(2,1)}), bf16[32,128,1024]{2,1,0:T(8,128)(2,1)}, u32[]{:S(2)}, u32[]{:S(2)}) async-start(bf16[32,128,1024]{2,1,0:T(8,128)(2,1)} %broadcast_select_fusion.1), calls=%async_computation | async-start | bytes 16777216 | tf_op jit(solution)/shard_map/all_to_all | solution.py:45
  35.0 38.4 %all-gather.4.cloned.1.call-done = bf16[2048,1024]{1,0:T(8,128)(2,1)} async-done(((bf16[256,1024]{1,0:T(8,128)(2,1)}), bf16[2048,1024]{1,0:T(8,128)(2,1)}) %all-gather.4.cloned.1.call-update) | async-done | bytes 4194320 | tf_op jit(solution)/shard_map/all_gather | solution.py:42
  73.4 148.9 %all-to-all-done = bf16[32,128,1024]{2,1,0:T(8,128)(2,1)} async-done(((bf16[32,128,1024]{2,1,0:T(8,128)(2,1)}), bf16[32,128,1024]{2,1,0:T(8,128)(2,1)}, u32[]{:S(2)}, u32[]{:S(2)}) %all-to-all-start) | async-done | bytes 8388640 | tf_op jit(solution)/shard_map/all_to_all | solution.py:45
  222.3 9.6 %pad_maximum_fusion = bf16[48,128,1024]{2,1,0:T(8,128)(2,1)} fusion(bf16[32,128,1024]{2,1,0:T(8,128)(2,1)} %all-to-all-done, bf16[16,128,1024]{2,1,0:T(8,128)(2,1)} %bitcast.34), kind=kLoop, calls=%fused_computation.46 | loop fusion | flops 6291456 | bytes 25165824 | tf_op jit(solution)/shard_map/concatenate | solution.py:46
  231.9 103.0 %while.28 = (s32[]{:T(128)}, f32[2,128,1024]{2,0,1:T(2,128)S(1)}, s32[64]{0:T(128)S(1)}, s32[]{:T(128)}, bf16[64,128,128]{2,1,0:T(8,128)(2,1)}, /*index=5*/s32[6...) while((s32[]{:T(128)}, f32[2,128,1024]{2,0,1:T(2,128)S(1)}, ...), condition=%wide.region_1.4_spmd.clone, body=%wide.region_0.3_spmd.clone.sunk | while | flops 274203744 | bytes 12849593 | solution.py:30
  232.7 5.3 gather_fusion
  245.6 5.3 gather_fusion
  258.4 5.3 gather_fusion
  271.3 5.3 gather_fusion
  284.2 5.3 gather_fusion
  297.0 5.3 gather_fusion
  309.9 5.3 gather_fusion
  322.8 5.3 gather_fusion
  342.3 7.5 %broadcast_select_fusion = bf16[32,128,1024]{2,1,0:T(8,128)(2,1)} fusion(bf16[32,128,1024]{2,1,0:T(8,128)(2,1)} %gather_fusion.3, pred[32]{0:T(512)(128)(4,1)S(1)} %compare_and_fusion.2), kind=kLoop, calls=%fused_computation.48 | loop fusion | flops 4194304 | bytes 16777248 | tf_op jit(solution)/shard_map/jit(_take)/select_n | solution.py:44
  349.8 10.2 %all-to-all-start.1 = ((bf16[32,128,1024]{2,1,0:T(8,128)(2,1)}), bf16[32,128,1024]{2,1,0:T(8,128)(2,1)}, u32[]{:S(2)}, u32[]{:S(2)}) async-start(bf16[32,128,1024]{2,1,0:T(8,128)(2,1)} %broadcast_select_fusion), calls=%async_computation.1 | async-start | bytes 16777216 | tf_op jit(solution)/shard_map/all_to_all | solution.py:45
  361.3 46.2 %all-gather.6.cloned.1.call-done = bf16[2048,1024]{1,0:T(8,128)(2,1)} async-done(((bf16[256,1024]{1,0:T(8,128)(2,1)}), bf16[2048,1024]{1,0:T(8,128)(2,1)}) %all-gather.6.cloned.1.call-update) | async-done | bytes 4194320 | tf_op jit(solution)/shard_map/all_gather | solution.py:42
  407.5 140.6 %all-to-all-done.1 = bf16[32,128,1024]{2,1,0:T(8,128)(2,1)} async-done(((bf16[32,128,1024]{2,1,0:T(8,128)(2,1)}), bf16[32,128,1024]{2,1,0:T(8,128)(2,1)}, u32[]{:S(2)}, u32[]{:S(2)}) %all-to-all-start.1) | async-done | bytes 8388640 | tf_op jit(solution)/shard_map/all_to_all | solution.py:45
  548.1 9.6 %pad_maximum_fusion.1 = bf16[48,128,1024]{2,1,0:T(8,128)(2,1)} fusion(bf16[32,128,1024]{2,1,0:T(8,128)(2,1)} %all-to-all-done.1, bf16[16,128,1024]{2,1,0:T(8,128)(2,1)} %bitcast.35), kind=kLoop, calls=%fused_computation.47 | loop fusion | flops 6291456 | bytes 25165824 | tf_op jit(solution)/shard_map/concatenate | solution.py:46
  557.7 109.0 %while.29 = (s32[]{:T(128)}, f32[2,128,1024]{2,0,1:T(2,128)}, s32[64]{0:T(128)S(1)}, s32[]{:T(128)}, bf16[64,128,128]{2,1,0:T(8,128)(2,1)}, /*index=5*/s32[64]{0...) while((s32[]{:T(128)}, f32[2,128,1024]{2,0,1:T(2,128)}, ...), condition=%wide.region_3.6_spmd.clone, body=%wide.region_2.0_spmd.clone.sunk | while | flops 274203744 | bytes 12849593 | solution.py:30
  558.4 5.3 gather_fusion.1
  612.8 5.3 gather_fusion.1
  669.4 49.6 %all-gather.8.cloned.1.call-done = bf16[2048,1024]{1,0:T(8,128)(2,1)} async-done(((bf16[256,1024]{1,0:T(8,128)(2,1)}), bf16[2048,1024]{1,0:T(8,128)(2,1)}) %all-gather.8.cloned.1.call-update) | async-done | bytes 4194320 | tf_op jit(solution)/shard_map/all_gather | solution.py:53
  (112 shorter events, 176.3 us)
Async XLA Ops:
  21.9 13.1 %copy-start.2 = (s32[256]{0:T(256)S(1)}, s32[256]{0:T(256)}, u32[]{:S(2)}) copy-start(s32[256]{0:T(256)} %param.16) | copy-start | bytes 3076
  21.9 200.4 %all-to-all-start = ((bf16[32,128,1024]{2,1,0:T(8,128)(2,1)}), bf16[32,128,1024]{2,1,0:T(8,128)(2,1)}, u32[]{:S(2)}, u32[]{:S(2)}) async-start(bf16[32,128,1024]{2,1,0:T(8,128)(2,1)} %broadcast_select_fusion.1), calls=%async_computation | async-start | bytes 16777216 | tf_op jit(solution)/shard_map/all_to_all | solution.py:45
  34.2 39.2 %all-gather.4.cloned.1.call-start = ((), (), s32[]{:S(2)}) async-start(), calls=%async_computation.2 | async-start | bytes 4718592 | tf_op jit(solution)/shard_map/all_gather | solution.py:42
  222.3 9.6 %copy-start.1 = (s32[64]{0:T(128)S(1)}, s32[64]{0:T(128)}, u32[]{:S(2)}) copy-start(s32[64]{0:T(128)} %param.19) | copy-start | bytes 772
  222.3 9.6 %copy-start.3 = (s32[64]{0:T(128)S(1)}, s32[64]{0:T(128)}, u32[]{:S(2)}) copy-start(s32[64]{0:T(128)} %param.18) | copy-start | bytes 772
  334.9 1.0 copy-start
  349.8 198.3 %all-to-all-start.1 = ((bf16[32,128,1024]{2,1,0:T(8,128)(2,1)}), bf16[32,128,1024]{2,1,0:T(8,128)(2,1)}, u32[]{:S(2)}, u32[]{:S(2)}) async-start(bf16[32,128,1024]{2,1,0:T(8,128)(2,1)} %broadcast_select_fusion), calls=%async_computation.1 | async-start | bytes 16777216 | tf_op jit(solution)/shard_map/all_to_all | solution.py:45
  360.0 47.4 %all-gather.6.cloned.1.call-start = ((), (), s32[]{:S(2)}) async-start(), calls=%async_computation.3 | async-start | bytes 4718592 | tf_op jit(solution)/shard_map/all_gather | solution.py:42
  361.0 357.9 %all-gather.8.cloned.1.call-start = ((), (), s32[]{:S(2)}) async-start(), calls=%async_computation.4 | async-start | bytes 4718592 | tf_op jit(solution)/shard_map/all_gather | solution.py:53
Sparse Core Ops, SparseCore 0:
  36.9 36.4 all-gather.3
  363.3 44.1 all-gather.5
  669.5 49.4 all-gather.7
where the time goes:
time: 729 us
  waiting for transfers between devices  424 us (58%)
  matrix products  118 us (16%)
  local copies, waits for them, and re-layouts  98.6 us (14%)
  other arithmetic  50.9 us (7%)
  starting transfers between devices  22.8 us (3%)
  between operations  13.8 us (2%)
    all_to_all x2, waiting for transfers between devices, body(): lax.all_to_all(outgoing, 'grp', split_axis=0, concat_axis=0, tiled=True)  290 us
    all_gather x2, waiting for transfers between devices, body(): gathered = lax.all_gather(current, 'row', axis=0, tiled=True)  84.6 us
    gather x16, local copies, waits for them, and re-layouts, add_block(): picked = jnp.take(sources, column_ids, axis=0)  84.1 us
    dot_general x16, matrix products, add_block(): return totals + jnp.einsum('rs,sif->rif', weights, products)  65.8 us
    all_gather x1, waiting for transfers between devices, body(): everyone = lax.all_gather(logs, 'row', axis=0, tiled=True)  49.6 us
    dot_general x16, matrix products, add_block(): jnp.einsum('sik,skf->sif', values_block, picked, preferred_element_type=j...  48.8 us
    all_to_all x2, starting transfers between devices, body(): lax.all_to_all(outgoing, 'grp', split_axis=0, concat_axis=0, tiled=True)  22.5 us
    concatenate x2, other arithmetic, body(): jnp.concatenate([gathered.reshape(-1, tile, width), incoming], axis=0)  19.2 us
  transfers between devices with their start and end apart: 5, of which 5 were waited for; matrix products, arithmetic and copies ran while one was open for 0% of the time, Pallas kernels for 0%

commit v1 on v0

v1 whole, which is shorter than its diff:
```python
import jax
import jax.numpy as jnp
from jax import lax
from jax.experimental import pallas as pl
from jax.experimental.pallas import tpu as pltpu
from jax.sharding import PartitionSpec as P

NX, NY, NZ = 4, 4, 8
TILE = 128
CHUNKS = 4
BACKLOG = 1.5
MESH = pl.DeviceIdType.MESH
SIGN = {"+": 1, "-": -1}


def build_kernel(rows_s, cols_s, count_s, send_s, degree_ref, values_hbm, row_ref, far_ref, bits_ref, div_ref, values, cells, sem):
    copy = pltpu.make_async_copy(values_hbm, values, sem)
    copy.start()
    codes = cells.shape[1]

    def clear(c, carry):
        for r in range(2):
            cells[r, c] = jnp.zeros((TILE, TILE), jnp.float32)
        return carry

    lax.fori_loop(0, codes, clear, 0)
    bits_ref[...] = jnp.zeros_like(bits_ref)
    for z in range(NZ):
        for y in range(NY):
            bit = send_s[0, y * NZ + z].astype(jnp.float32)
            bits_ref[z, pl.ds(y, 1), :] = jnp.full((1, TILE), bit, jnp.float32)
    for h in range(2):
        degrees = degree_ref[pl.ds(h, 1), :].astype(jnp.float32)
        div_ref[pl.ds(h * TILE, TILE), :] = jnp.broadcast_to(degrees, (TILE, TILE)).T
    copy.wait()

    def add(s, carry):
        r, c = rows_s[s], cols_s[s]
        cells[r, c] = cells[r, c] + values[s].astype(jnp.float32)
        return carry

    lax.fori_loop(0, count_s[0], add, 0)
    local = codes - NY * NZ
    for r in range(2):
        rows = pl.ds(r * TILE, TILE)
        for c in range(local):
            row_ref[rows, pl.ds(c * TILE, TILE)] = cells[r, c].astype(jnp.bfloat16)
        for y in range(NY):
            for z in range(NZ):
                far_ref[y, rows, pl.ds(z * TILE, TILE)] = cells[r, local + y * NZ + z].astype(jnp.bfloat16)


def build_dense(tile_rows, tile_cols, tile_count, send_tiles, degree, tile_values):
    slots = tile_values.shape[0]
    codes = 2 * 2 * NX + NY * NZ
    smem = pl.BlockSpec(memory_space=pltpu.SMEM)
    vmem = pl.BlockSpec(memory_space=pltpu.VMEM)
    return pl.pallas_call(
        build_kernel,
        out_shape=(
            jax.ShapeDtypeStruct((2 * TILE, 4 * NX * TILE), jnp.bfloat16),
            jax.ShapeDtypeStruct((NY, 2 * TILE, NZ * TILE), jnp.bfloat16),
            jax.ShapeDtypeStruct((NZ, 8, TILE), jnp.float32),
            jax.ShapeDtypeStruct((2 * TILE, TILE), jnp.float32),
        ),
        in_specs=[smem, smem, smem, smem, vmem, pl.BlockSpec(memory_space=pl.ANY)],
        out_specs=(vmem, vmem, vmem, vmem),
        scratch_shapes=[
            pltpu.VMEM((slots, TILE, TILE), jnp.bfloat16),
            pltpu.VMEM((2, codes, TILE, TILE), jnp.float32),
            pltpu.SemaphoreType.DMA,
        ],
        compiler_params=pltpu.CompilerParams(vmem_limit_bytes=24 * 1024 * 1024),
    )(tile_rows, tile_cols, tile_count, send_tiles, degree.reshape(2, TILE), tile_values)


def task_list(chunks, width):
    tasks = {}
    part = 1.0 / chunks

    def task(name, deps, link=None, units=0.0, cost=0.05, rank=0):
        tasks[name] = (deps, link, units, cost, rank)

    def got(name):
        return ("got", name)

    for k in range(1, NZ):
        task(("B", k), [], "z+", 0.01, 0.05, -20)
    for d in "+-":
        task(("W2a", d), [], "y" + d, 1, 0.05, -11)
        task(("W1", d), [], "y" + d, 2, 0.05, -10)
        task(("W2b", d), [got(("W2a", d))], "y" + d, 1, 0.05, -10)
    bits = [got(("B", k)) for k in range(1, NZ)]
    task(("E", "0"), bits, None, 0, 0.8, -5)
    task(("E", "+"), bits + [got(("W1", "-"))], None, 0, 0.8, -5)
    task(("E", "-"), bits + [got(("W1", "+"))], None, 0, 0.8, -5)
    task(("E", "2"), bits + [got(("W2b", "+")), got(("W2b", "-"))], None, 0, 0.8, -5)
    product = 2 * (2 * TILE) * (NZ * 2 * TILE) * width / 800e6
    gram_deps = []
    for p in range(3):
        for c in range(chunks):
            rank = p * chunks + c
            own = [("L", c)] if p == 0 else [("F", p - 1, c)]
            if p == 0:
                task(("L", c), [], None, 0, 0.05, rank)

            def ring(kind, axis, size):
                half = size // 2
                for d in "+-":
                    for s in range(1, half + 1):
                        deps = own if s == 1 else [got((kind, p, c, d, s - 1))]
                        task((kind, p, c, d, s), deps, axis + d, (2 if s < half else 1) * part, 0.05, rank)
                return [got((kind, p, c, d, s)) for d in "+-" for s in range(1, half + 1)]

            column = ring("Z", "z", NZ) + own if p < 2 else []
            row = ring("X", "x", NX) + own
            for q, deps, units in (
                ("0", own, 2),
                ("+", [got(("X", p, c, "+", 1))], 2),
                ("-", [got(("X", p, c, "-", 1))], 2),
                ("p", [got(("X", p, c, "+", 2))], 1),
                ("m", [got(("X", p, c, "-", 2))], 1),
            ):
                task(("D", p, c, q), deps, "d", units * part, 0.05, rank)
                row.append(got(("D", p, c, q)))
            if p == 2:
                gram_deps += row
                continue
            for j in "2+-0":
                task(("C", p, c, j), column + [("E", j)], None, 0, product, rank)
            task(("R", p, c), row + [("C", p, c, "0")], None, 0, product, rank)
            arrived = []
            for d in "+-":
                task(("Y1", p, c, d), [("C", p, c, "2")], "y" + d, part, 0.05, rank)
                task(("YB", p, c, d), [("C", p, c, d)], "y" + d, part, 0.05, rank)
                task(("A", p, c, d), [got(("Y1", p, c, d)), ("C", p, c, d)], None, 0, 0.3 * part * 2, rank)
                task(("YA", p, c, d), [("A", p, c, d)], "y" + d, part, 0.05, rank)
                arrived += [got(("YB", p, c, d)), got(("YA", p, c, d))]
            task(("F", p, c), arrived + [("R", p, c)] + own, None, 0, 1.6 * part, rank)
    task(("G",), gram_deps, None, 0, 2.0, 99)
    return tasks


def task_order(tasks, backlog):
    unit, latency = 5.62, {"d": 1.0}
    now, free, ended, landed, order = 3.0, {}, {}, {}, []
    left = dict(tasks)
    while left:
        best, best_key, soonest = None, None, 1e9
        for name, (deps, link, units, cost, rank) in left.items():
            ready = 0.0
            for dep in deps:
                at = landed.get(dep[1]) if dep[0] == "got" else ended.get(dep)
                if at is None:
                    ready = None
                    break
                ready = max(ready, at)
            if ready is None:
                continue
            if link is not None:
                ready = max(ready, free.get(link, 0.0) - backlog)
            if ready <= now + 1e-9:
                key = (link is None, rank, ready)
                if best is None or key < best_key:
                    best, best_key = name, key
            else:
                soonest = min(soonest, ready)
        if best is None:
            now = soonest
            continue
        deps, link, units, cost, rank = left.pop(best)
        now += cost
        ended[best] = now
        if link is not None:
            took = units * unit * (0.07 if link == "d" else 1.0)
            free[link] = max(now, free.get(link, 0.0)) + took
            landed[best] = free[link] + latency.get(link, 2.0)
        order.append(best)
    return order, now


def step_kernel(tasks, order, width, block_hbm, row_ref, far_ref, bits_ref, div_ref, logs_hbm, gram_ref,
                xz, xr, lg, wide, wr, stage, bits, p2, ps, pf, y1, yr, acc, flip, load_sem, out_sem, send_sem, recv_sem):
    chunks = xz.shape[1]
    g, r = lax.axis_index("grp"), lax.axis_index("row")
    me = (lax.div(g, NZ), lax.rem(g, NZ), lax.div(r, 2), lax.rem(r, 2))

    def moved(at, axis, by):
        y, z, x, k = at
        if axis == "y":
            return (lax.rem(y + by + NY, NY), z, x, k)
        if axis == "z":
            return (y, lax.rem(z + by + NZ, NZ), x, k)
        if axis == "x":
            return (y, z, lax.rem(x + by + NX, NX), k)
        return (y, z, x, 1 - k)

    def device(at):
        return (at[0] * NZ + at[1], at[2] * 2 + at[3])

    def rows(first, size):
        return pl.ds(pl.multiple_of(first, TILE), size)

    number = {}
    for name in tasks:
        if tasks[name][1] is not None:
            number[name] = len(number)

    def target(name, at):
        kind = name[0]
        if kind == "B":
            return moved(at, "z", name[1])
        if kind == "D":
            return moved(at, "k", 1)
        axis = {"Z": "z", "X": "x"}.get(kind, "y")
        return moved(at, axis, SIGN[name[1] if kind[0] == "W" else name[3]])

    def source(name, at):
        kind = name[0]
        if kind == "B":
            return moved(at, "z", -name[1])
        if kind == "D":
            return moved(at, "k", 1)
        axis = {"Z": "z", "X": "x"}.get(kind, "y")
        return moved(at, axis, -SIGN[name[1] if kind[0] == "W" else name[3]])

    def span(first, half):
        if half is None:
            return rows(first, 2 * TILE)
        return rows(first + half * TILE, TILE)

    def ends(name, at):
        kind = name[0]
        if kind == "B":
            return bits_ref.at[moved(at, "z", name[1])[1]], bits.at[at[1]]
        if kind == "W1":
            d = name[1]
            return far_ref.at[moved(at, "y", SIGN[d])[0]], wr.at[0 if d == "-" else 1]
        if kind == "W2a":
            h = 0 if name[1] == "+" else 1
            return far_ref.at[moved(at, "y", 2)[0], pl.ds(h * TILE, TILE)], stage.at[h]
        if kind == "W2b":
            h = 0 if name[1] == "+" else 1
            return stage.at[h], wr.at[2, pl.ds(h * TILE, TILE)]
        p, c, d = name[1:4]
        if kind == "Z":
            s = name[4]
            first = moved(at, "z", -SIGN[d] * (s - 1))[1] * (2 * TILE)
            half = None if s < NZ // 2 else (0 if d == "+" else 1)
            ref = xz.at[p, c, span(first, half)]
            return ref, ref
        if kind in "XD":
            whole = xr.at[p] if p < 2 else lg
            if kind == "X":
                s = name[4]
                from_x = moved(at, "x", -SIGN[d] * (s - 1))[2]
                half = None if s < NX // 2 else (0 if d == "+" else 1)
            else:
                by, half = {"0": (0, None), "+": (-1, None), "-": (1, None), "p": (-2, 0), "m": (2, 1)}[d]
                from_x = moved(at, "x", by)[2]
            ref = whole.at[c, span((from_x * 2 + at[3]) * (2 * TILE), half)]
            return ref, ref
        i = 0 if d == "+" else 1
        top, low = pl.ds(i * TILE, TILE), pl.ds((1 - i) * TILE, TILE)
        if kind == "Y1":
            return p2.at[p, c, top], y1.at[p, c, i]
        if kind == "YA":
            return ps.at[p, c, i, top], yr.at[p, c, i, top]
        return ps.at[p, c, i, low], yr.at[p, c, i, low]

    def descriptor(name, at, to):
        src, dst = ends(name, at)
        i = number[name]
        return pltpu.make_async_remote_copy(
            src_ref=src, dst_ref=dst, send_sem=send_sem.at[i], recv_sem=recv_sem.at[i],
            device_id=device(to), device_id_type=MESH)

    def arrival(name):
        origin = source(name, me)
        dst = ends(name, origin)[1]
        i = number[name]
        return pltpu.make_async_remote_copy(
            src_ref=dst, dst_ref=dst, send_sem=send_sem.at[i], recv_sem=recv_sem.at[i],
            device_id=device(origin), device_id_type=MESH)

    own_z = rows(me[1] * (2 * TILE), 2 * TILE)
    own_r = rows(r * (2 * TILE), 2 * TILE)

    def loads(c):
        piece = block_hbm.at[:, pl.ds(c * width, width)]
        return (pltpu.make_async_copy(piece, xz.at[0, c, own_z], load_sem.at[c, 0]),
                pltpu.make_async_copy(piece, xr.at[0, c, own_r], load_sem.at[c, 1]))

    def store(c):
        return pltpu.make_async_copy(lg.at[c, own_r], logs_hbm.at[:, pl.ds(c * width, width)], out_sem.at[c])

    for c in range(chunks):
        for copy in loads(c):
            copy.start()
    bits[me[1]] = bits_ref[me[1]]
    peers = [moved(me, "z", k) for k in range(1, NZ)]
    peers += [moved(me, "y", 1), moved(me, "y", -1), moved(me, "x", 1), moved(me, "x", -1), moved(me, "k", 1)]
    barrier = pltpu.get_barrier_semaphore()
    for peer in peers:
        pl.semaphore_signal(barrier, inc=1, device_id=device(peer), device_id_type=MESH)
    pl.semaphore_wait(barrier, len(peers))

    def dot(a, b):
        return jnp.dot(a, b, preferred_element_type=jnp.float32)

    def widen(j):
        slot = "0+-2".index(j)
        y = moved(me, "y", {"0": 0, "+": 1, "-": -1, "2": 2}[j])[0]
        for z in range(NZ):
            bit = bits[z, pl.ds(y, 1), :]
            if j == "0":
                piece = far_ref[me[0], :, pl.ds(z * TILE, TILE)]
            else:
                piece = wr[slot - 1, :, pl.ds(z * TILE, TILE)]
            piece = piece.astype(jnp.float32)
            wide[slot, :, pl.ds(z * 2 * TILE, TILE)] = (piece * (1.0 - bit)).astype(jnp.bfloat16)
            wide[slot, :, pl.ds(z * 2 * TILE + TILE, TILE)] = (piece * bit).astype(jnp.bfloat16)

    def run(name):
        kind = name[0]
        if kind == "L":
            for copy in loads(name[1]):
                copy.wait()
        elif kind == "E":
            widen(name[1])
        elif kind == "C":
            p, c, j = name[1:]
            made = dot(wide["0+-2".index(j)], xz[p, c])
            if j == "0":
                acc[p, c] = made
            elif j == "2":
                p2[p, c] = made.astype(jnp.bfloat16)
            else:
                i = 0 if j == "+" else 1
                pf[p, c, i] = made[i * TILE:(i + 1) * TILE]
                ps[p, c, i, pl.ds((1 - i) * TILE, TILE)] = made[(1 - i) * TILE:(2 - i) * TILE].astype(jnp.bfloat16)
        elif kind == "R":
            p, c = name[1:]
            acc[p, c] += dot(row_ref[...], xr[p, c])
        elif kind == "A":
            p, c, d = name[1:]
            i = 0 if d == "+" else 1
            ps[p, c, i, pl.ds(i * TILE, TILE)] = (pf[p, c, i] + y1[p, c, i].astype(jnp.float32)).astype(jnp.bfloat16)
        elif kind == "F":
            p, c = name[1:]
            summed = acc[p, c] + yr[p, c, 0].astype(jnp.float32) + yr[p, c, 1].astype(jnp.float32)
            divisor = jnp.concatenate([div_ref[...]] * (width // TILE), axis=1)
            power = (summed / divisor).astype(jnp.bfloat16)
            if p == 0:
                xz[1, c, own_z] = power
                xr[1, c, own_r] = power
            else:
                total = xr[1, c, own_r].astype(jnp.float32) + power.astype(jnp.float32)
                lg[c, own_r] = jnp.log(jnp.maximum(3.0 * total, 1.0)).astype(jnp.bfloat16)
                store(c).start()
        else:
            per = width // TILE
            mine = pl.ds(pl.multiple_of(lax.rem(r, per) * TILE, TILE), TILE)
            flip[...] = lg[lax.div(r, per), :, mine].T
            for c in range(chunks):
                gram_ref[:, pl.ds(c * width, width)] = dot(flip[...], lg[c]) * (1.0 / (lg.shape[1]))

    waited = set()
    for name in order:
        for dep in tasks[name][0]:
            if dep[0] == "got" and dep[1] not in waited:
                waited.add(dep[1])
                arrival(dep[1]).wait_recv()
        if name in number:
            descriptor(name, me, target(name, me)).start()
        else:
            run(name)
    for c in range(chunks):
        store(c).wait()
    for name in number:
        descriptor(name, me, target(name, me)).wait_send()


def body(block, degree, tile_values, tile_rows, tile_cols, tile_count, send_tiles):
    near, far, bits, divisor = build_dense(tile_rows, tile_cols, tile_count, send_tiles, degree, tile_values)
    rows_here, features = block.shape
    chunks = CHUNKS
    width = features // chunks
    tasks = task_list(chunks, width)
    order, _ = task_order(tasks, BACKLOG)
    sends = sum(1 for t in tasks.values() if t[1] is not None)
    vmem = pl.BlockSpec(memory_space=pltpu.VMEM)
    hbm = pl.BlockSpec(memory_space=pl.ANY)
    column = NZ * 2 * TILE
    bf16, f32 = jnp.bfloat16, jnp.float32
    ranks = 2 * NX

    def kernel(*refs):
        step_kernel(tasks, order, width, *refs)

    return pl.pallas_call(
        kernel,
        out_shape=(
            jax.ShapeDtypeStruct((rows_here, features), bf16),
            jax.ShapeDtypeStruct((features // ranks, features), f32),
        ),
        in_specs=[hbm, vmem, vmem, vmem, vmem],
        out_specs=(hbm, vmem),
        scratch_shapes=[
            pltpu.VMEM((2, chunks, column, width), bf16),
            pltpu.VMEM((2, chunks, ranks * 2 * TILE, width), bf16),
            pltpu.VMEM((chunks, ranks * 2 * TILE, width), bf16),
            pltpu.VMEM((4, 2 * TILE, column), bf16),
            pltpu.VMEM((3, 2 * TILE, NZ * TILE), bf16),
            pltpu.VMEM((2, TILE, NZ * TILE), bf16),
            pltpu.VMEM((NZ, 8, TILE), f32),
            pltpu.VMEM((2, chunks, 2 * TILE, width), bf16),
            pltpu.VMEM((2, chunks, 2, 2 * TILE, width), bf16),
            pltpu.VMEM((2, chunks, 2, TILE, width), f32),
            pltpu.VMEM((2, chunks, 2, TILE, width), bf16),
            pltpu.VMEM((2, chunks, 2, 2 * TILE, width), bf16),
            pltpu.VMEM((2, chunks, 2 * TILE, width), f32),
            pltpu.VMEM((TILE, ranks * 2 * TILE), bf16),
            pltpu.SemaphoreType.DMA((chunks, 2)),
            pltpu.SemaphoreType.DMA((chunks,)),
            pltpu.SemaphoreType.DMA((sends,)),
            pltpu.SemaphoreType.DMA((sends,)),
        ],
        compiler_params=pltpu.CompilerParams(
            collective_id=0, has_side_effects=True, vmem_limit_bytes=52 * 1024 * 1024),
    )(block, near, far, bits, divisor)


def solution(mesh):
    placed = (
        P(("grp", "row"), None),
        P(("grp", "row")),
        P(("grp", "row"), None, None),
        P(("grp", "row")),
        P(("grp", "row")),
        P(("grp", "row")),
        P(("grp", "row"), None),
    )
    return jax.shard_map(
        body,
        mesh=mesh,
        in_specs=placed,
        out_specs=(P(("grp", "row"), None), P(("grp", "row"), None)),
        check_vma=False,
    )
```

time: 729 us -> 139 us (0.19)
  waiting for transfers between devices: 424 us -> 0 us
  Pallas kernels: 0 us -> 130 us
  matrix products: 118 us -> 0 us
  local copies, waits for them, and re-layouts: 98.6 us -> 8.13 us
  other arithmetic: 50.9 us -> 0 us
  starting transfers between devices: 22.8 us -> 0 us
  between operations: 13.8 us -> 1.32 us
    all_to_all x2 -> x0, waiting for transfers between devices: 290 us -> none  [body(): lax.all_to_all(outgoing, 'grp', split_axis=0, concat_axis=0, tiled=True)]
    all_gather x3 -> x0, waiting for transfers between devices: 134 us -> none  [the longest x2 84.6 us: body(): gathered = lax.all_gather(current, 'row', axis=0, tiled=True)]
    pallas_call x0 -> x2, Pallas kernels: none -> 130 us  [the longest x1 127 us: body(): pl.pallas_call(kernel, out_shape=(jax.ShapeDtypeStruct((rows_here, featur...]
    dot_general x33 -> x0, matrix products: 118 us -> none  [the longest x16 65.8 us: add_block(): return totals + jnp.einsum('rs,sif->rif', weights, products)]
    gather x18 -> x0, local copies, waits for them, and re-layouts: 94.8 us -> none  [the longest x16 84.1 us: add_block(): picked = jnp.take(sources, column_ids, axis=0)]
    all_to_all x2 -> x0, starting transfers between devices: 22.5 us -> none  [body(): lax.all_to_all(outgoing, 'grp', split_axis=0, concat_axis=0, tiled=True)]
    concatenate x2 -> x0, other arithmetic: 19.2 us -> none  [body(): jnp.concatenate([gathered.reshape(-1, tile, width), incoming], axis=0)]
    select_n x3 -> x0, other arithmetic: 15.7 us -> none  [body(): outgoing = jnp.take(own_tiles, send_tiles[0], axis=0)]
  transfers between devices with their start and end apart: 5 -> 0, of which waited for: 5 -> 0; matrix products, arithmetic and copies ran while one was open for 0% -> 0% of each run, Pallas kernels for 0% -> 0%
where the time goes in v1:
time: 139 us
  Pallas kernels  130 us (94%)
  local copies, waits for them, and re-layouts  8.13 us (6%)
    pallas_call x1, Pallas kernels, body(): pl.pallas_call(kernel, out_shape=(jax.ShapeDtypeStruct((rows_here, featur...  127 us
    unnamed x18, local copies, waits for them, and re-layouts  8.13 us

profile of v1, /device:TPU:1, one launch (start us, length us, event | category | flops | bytes accessed | tf_op | source)
XLA Modules:
  0.0 139.0 jit_solution(5010619700612399629)
XLA Ops:
  1.3 0.0 copy-start
  1.3 1.6 %copy-done = bf16[64,128,128]{2,1,0:T(8,128)(2,1)S(1)} copy-done((bf16[64,128,128]{2,1,0:T(8,128)(2,1)S(1)}, bf16[64,128,128]{2,1,0:T(8,128)(2,1)}, u32[]{:S(2)}) %copy-start) | copy-done | bytes 2097176
  2.9 0.0 copy-start.4
  2.9 0.7 copy-done.4
  3.5 0.0 copy-start.5
  3.6 0.7 copy-done.5
  4.2 0.0 copy-start.6
  4.2 0.7 copy-done.6
  4.9 0.0 copy-start.7
  4.9 0.7 copy-done.7
  5.5 0.0 copy-start.3
  5.5 2.2 %shard_map.86 = (bf16[256,2048]{1,0:T(8,128)(2,1)S(1)}, bf16[4,256,1024]{2,1,0:T(8,128)(2,1)S(1)}, f32[8,8,128]{2,1,0:T(8,128)S(1)}, f32[256,128]{1,0:T(8,128)S(1)}) custom-call(s32[64]{0:T(128)S(1)} %copy-done.5, s32[64]{0:T(128)S(1)} %copy-done.6, s32[1]{0:T(128)S(6)} %copy.11.count_s, s32[1,32]{1,0:T(1,128)S(1)} %copy-done.7, s32[2,128]{1,0:T(2,128)S(1)} %bitcast.1, ...), custom_call_target="tpu_custom_call" | custom-call | tf_op jit(solution)/shard_map/pallas_call | solution.py:58
  7.7 0.0 copy-start.1
  7.7 1.3 copy-done.1
  9.1 0.0 copy-start.2
  9.1 1.0 copy-done.2
  10.0 0.0 copy-done.3
  10.1 127.3 %shard_map.87 = (bf16[256,1024]{1,0:T(8,128)(2,1)S(1)}, f32[128,1024]{1,0:T(8,128)S(1)}) custom-call(bf16[256,1024]{1,0:T(8,128)(2,1)S(1)} %copy-done.3, bf16[256,2048]{1,0:T(8,128)(2,1)} %copy-done.2, bf16[4,256,1024]{2,1,0:T(8,128)(2,1)} %copy-done.1, f32[8,8,128]{2,1,0:T(8,128)S(1)} %get-tuple-element.8.refs_3_, f32[256,128]{1,0:T(8,128)S(1)} %get-tuple-element.9.refs_4_), custom_call_target="tpu_custom_call" | custom-call | tf_op jit(solution)/shard_map/pallas_call | solution.py:401
  137.4 0.8 copy.12
  138.2 0.8 copy.13
Async XLA Ops:
  1.3 1.6 %copy-start = (bf16[64,128,128]{2,1,0:T(8,128)(2,1)S(1)}, bf16[64,128,128]{2,1,0:T(8,128)(2,1)}, u32[]{:S(2)}) copy-start(bf16[64,128,128]{2,1,0:T(8,128)(2,1)} %values_hbm.1) | copy-start | bytes 6291460
  2.9 0.7 copy-start.4
  3.5 0.7 copy-start.5
  4.2 0.7 copy-start.6
  4.9 0.7 copy-start.7
  5.5 4.5 %copy-start.3 = (bf16[256,1024]{1,0:T(8,128)(2,1)S(1)}, bf16[256,1024]{1,0:T(8,128)(2,1)}, u32[]{:S(2)}) copy-start(bf16[256,1024]{1,0:T(8,128)(2,1)} %refs_0_.1) | copy-start | bytes 1572868
  7.7 1.3 copy-start.1
  9.1 1.0 copy-start.2

commit v2 on v1

v2 whole, which is shorter than its diff:
```python
import jax
import jax.numpy as jnp
from jax import lax
from jax.experimental import pallas as pl
from jax.experimental.pallas import tpu as pltpu
from jax.sharding import PartitionSpec as P

NX, NY, NZ = 4, 4, 8
TILE = 128
WIDTHS = (256, 256, 256, 128, 128)
BACKLOG = 0.5
RATE = 460e6
LIMIT = 46 * 1024 * 1024
BUILD_LIMIT = 20 * 1024 * 1024
BITS_LATE = 4.0
LATE = {"z": 2.3, "y": 2.8, "x": 5.0, "d": 4.0, "X": 2.5, "D": 1.5}
MESH = pl.DeviceIdType.MESH
ORDER = (
    48, 53, 49, 8, 18, 19, 23, 78, 0, 108, 11, 4, 83, 50, 59, 121, 9, 27, 12, 1, 5, 24, 20, 113, 7, 61, 54, 13,
    138, 87, 57, 139, 89, 2, 10, 79, 21, 25, 119, 29, 3, 143, 6, 93, 63, 55, 51, 120, 22, 26, 80, 149, 15, 91, 28, 84,
    117, 31, 32, 90, 140, 30, 56, 144, 52, 16, 58, 17, 35, 62, 43, 147, 39, 109, 14, 36, 85, 81, 141, 44, 150, 40, 65, 73,
    69, 88, 60, 41, 45, 122, 42, 114, 46, 110, 34, 66, 74, 153, 33, 70, 145, 37, 86, 71, 64, 82, 38, 75, 72, 76, 115, 142,
    47, 111, 172, 92, 67, 146, 168, 176, 68, 118, 77, 205, 201, 152, 197, 148, 94, 95, 116, 96, 103, 104, 112, 124, 151, 99, 173, 207,
    155, 100, 157, 169, 156, 163, 202, 177, 160, 198, 127, 105, 125, 106, 101, 129, 102, 126, 159, 174, 133, 170, 97, 98, 165, 203, 166, 199,
    178, 180, 107, 164, 135, 130, 208, 206, 161, 131, 154, 226, 230, 234, 236, 162, 211, 171, 136, 132, 210, 158, 175, 167, 284, 288, 123, 134,
    200, 292, 128, 204, 137, 231, 227, 184, 188, 240, 294, 192, 185, 259, 255, 293, 237, 179, 193, 189, 285, 213, 221, 181, 217, 289, 214, 232,
    222, 228, 235, 194, 182, 265, 260, 190, 191, 298, 256, 212, 195, 183, 215, 219, 218, 223, 290, 238, 263, 295, 286, 224, 209, 220, 269, 186,
    233, 229, 187, 196, 241, 261, 257, 216, 313, 266, 225, 291, 287, 315, 242, 250, 246, 243, 323, 258, 247, 262, 251, 321, 244, 239, 300, 308,
    304, 301, 248, 249, 252, 253, 264, 271, 279, 316, 314, 275, 305, 325, 319, 299, 272, 310, 309, 267, 297, 324, 296, 322, 311, 306, 307, 276,
    280, 268, 245, 254, 331, 329, 281, 282, 277, 278, 270, 326, 302, 273, 327, 303, 312, 320, 347, 345, 274, 333, 283, 339, 337, 330, 317, 318,
    332, 348, 346, 340, 338, 334, 342, 341, 350, 336, 349, 351, 335, 343, 328, 352, 344, 353,
)
SIGN = {"+": 1, "-": -1}


def build_kernel(cell_s, count_s, values, row_ref, far_ref, cells):
    codes = cells.shape[0] // 2

    def clear(c, carry):
        for r in range(2):
            cells[r * codes + c] = jnp.zeros((TILE, TILE), jnp.float32)
        return carry

    lax.fori_loop(0, codes, clear, 0)

    def add(s, carry):
        cell = cell_s[s]
        cells[cell] = cells[cell] + values[s].astype(jnp.float32)
        return carry

    lax.fori_loop(0, count_s[0], add, 0)
    local = codes - NY * NZ
    for r in range(2):
        rows = pl.ds(r * TILE, TILE)
        for c in range(local):
            row_ref[rows, pl.ds(c * TILE, TILE)] = cells[r * codes + c].astype(jnp.bfloat16)
        for y in range(NY):
            for z in range(NZ):
                far_ref[y, rows, pl.ds(z * TILE, TILE)] = cells[r * codes + local + y * NZ + z].astype(jnp.bfloat16)


def build_dense(tile_rows, tile_cols, tile_count, tile_values):
    codes = 2 * 2 * NX + NY * NZ
    smem = pl.BlockSpec(memory_space=pltpu.SMEM)
    vmem = pl.BlockSpec(memory_space=pltpu.VMEM)
    return pl.pallas_call(
        build_kernel,
        out_shape=(
            jax.ShapeDtypeStruct((2 * TILE, 4 * NX * TILE), jnp.bfloat16),
            jax.ShapeDtypeStruct((NY, 2 * TILE, NZ * TILE), jnp.bfloat16),
        ),
        in_specs=[smem, smem, vmem],
        out_specs=(vmem, vmem),
        scratch_shapes=[pltpu.VMEM((2 * codes, TILE, TILE), jnp.float32)],
        compiler_params=pltpu.CompilerParams(vmem_limit_bytes=BUILD_LIMIT),
    )(tile_rows * codes + tile_cols, tile_count, tile_values)


def task_list(widths):
    tasks = {}
    chunks = len(widths)

    def task(name, deps, link=None, units=0.0, cost=0.05, rank=0):
        late = LATE.get("X" if name[0] == "X" and name[1] == 2 else "D" if name[0] == "D" and name[1] == 2 else (link or "z")[0])
        late = BITS_LATE if name[0] == "B" else late
        tasks[name] = (deps, link, units, cost, rank, late)

    def got(name):
        return ("got", name)

    hops = [("B", d, s) for d in "+-" for s in range(1, NZ // 2 + (d == "+"))]
    for _, d, s in hops:
        task(("B", d, s), [] if s == 1 else [got(("B", d, s - 1))], "z" + d, 0.01, 0.05, -20)
    task(("H",), [], None, 0, 0.3, 50)
    for d in "+-":
        task(("W2a", d), [], "y" + d, 1, 0.05, -11)
        task(("W1", d), [], "y" + d, 2, 0.05, -10)
        task(("W2b", d), [got(("W2a", d))], "y" + d, 1, 0.05, -10)
    bits = [got(hop) for hop in hops] + [("H",)]
    task(("E", "0"), bits, None, 0, 0.4, -5)
    task(("E", "+"), bits + [got(("W1", "-"))], None, 0, 0.4, -5)
    task(("E", "-"), bits + [got(("W1", "+"))], None, 0, 0.4, -5)
    task(("E", "2"), bits + [got(("W2b", "+")), got(("W2b", "-"))], None, 0, 0.4, -5)
    gram_deps = []
    for p in range(3):
        for c in range(chunks):
            rank = p * chunks + c
            part = widths[c] / sum(widths)
            product = 2 * (2 * TILE) * (NZ * 2 * TILE) * max(widths[c], 192) / RATE
            own = [("L", c)] if p == 0 else [("F", p - 1, c)]
            if p == 0:
                task(("L", c), [], None, 0, 0.05, rank)

            def ring(kind, axis, size):
                half = size // 2
                for d in "+-":
                    for s in range(1, half + 1):
                        deps = own if s == 1 else [got((kind, p, c, d, s - 1))]
                        task((kind, p, c, d, s), deps, axis + d, (2 if s < half else 1) * part, 0.05, rank)
                return [got((kind, p, c, d, s)) for d in "+-" for s in range(1, half + 1)]

            column = ring("Z", "z", NZ) + own if p < 2 else []
            row = ring("X", "x", NX) + own
            for q, deps, units in (
                ("0", own, 2),
                ("+", [got(("X", p, c, "+", 1))], 2),
                ("-", [got(("X", p, c, "-", 1))], 2),
                ("f", [got(("X", p, c, "+", 2)), got(("X", p, c, "-", 2))], 2),
            ):
                task(("D", p, c, q), deps, "d", units * part, 0.05, rank)
                row.append(got(("D", p, c, q)))
            if p == 2:
                gram_deps += row
                continue
            task(("C", p, c, "2"), column + [("E", "2")], None, 0, product, rank)
            task(("C", p, c, "s"), column + [("E", j) for j in "+-"], None, 0, 2.1 * product, rank)
            task(("C", p, c, "0"), column + [("E", "0")], None, 0, product * 0.95, rank)
            task(("R", p, c), row + [("C", p, c, "0"), ("H",)], None, 0, product * 1.2, rank)
            arrived = []
            for d in "+-":
                task(("Y1", p, c, d), [("C", p, c, "2")], "y" + d, part, 0.05, rank)
                task(("YB", p, c, d), [("C", p, c, "s")], "y" + d, part, 0.05, rank)
                task(("A", p, c, d), [got(("Y1", p, c, d)), ("C", p, c, "s")], None, 0, 0.05, rank)
                task(("YA", p, c, d), [("A", p, c, d)], "y" + d, part, 0.05, rank)
                arrived += [got(("YB", p, c, d)), got(("YA", p, c, d))]
            task(("F", p, c), arrived + [("R", p, c), ("H",)] + own, None, 0, 0.15, rank)
    task(("G",), gram_deps, None, 0, 0.95, 99)
    return tasks


def task_order(tasks, backlog):
    unit = 5.62
    now, free, ended, landed, order = 3.0, {}, {}, {}, []
    left = dict(tasks)
    while left:
        best, best_key, soonest = None, None, 1e9
        for name, (deps, link, units, cost, rank, late) in left.items():
            ready = 0.0
            for dep in deps:
                at = landed.get(dep[1]) if dep[0] == "got" else ended.get(dep)
                if at is None:
                    ready = None
                    break
                ready = max(ready, at)
            if ready is None:
                continue
            if link is not None:
                ready = max(ready, free.get(link, 0.0) - backlog)
            if ready <= now + 1e-9:
                key = (link is None, rank, ready)
                if best is None or key < best_key:
                    best, best_key = name, key
            else:
                soonest = min(soonest, ready)
        if best is None:
            now = soonest
            continue
        deps, link, units, cost, rank, late = left.pop(best)
        now += cost
        ended[best] = now
        if link is not None:
            took = units * unit * (0.07 if link == "d" else 1.0)
            free[link] = max(now, free.get(link, 0.0)) + took
            landed[best] = free[link] + late
        order.append(best)
    return order, now


def step_kernel(tasks, order, widths, block_hbm, row_ref, far_ref, send_hbm, degree_hbm, logs_hbm, gram_hbm,
                per_chunk, wide, wr, stage, bits, flip, send_ref, degree_ref, div_ref, gram_ref,
                load_sem, misc_sem, out_sem, send_sem, recv_sem):
    chunks = len(widths)
    offsets = [sum(widths[:c]) for c in range(chunks)]
    xz, xr, p2, ps, pf, y1, yr, acc, lg = per_chunk
    g, r = lax.axis_index("grp"), lax.axis_index("row")
    me = (lax.div(g, NZ), lax.rem(g, NZ), lax.div(r, 2), lax.rem(r, 2))

    def moved(at, axis, by):
        y, z, x, k = at
        if axis == "y":
            return (lax.rem(y + by + NY, NY), z, x, k)
        if axis == "z":
            return (y, lax.rem(z + by + NZ, NZ), x, k)
        if axis == "x":
            return (y, z, lax.rem(x + by + NX, NX), k)
        return (y, z, x, 1 - k)

    def device(at):
        return (at[0] * NZ + at[1], at[2] * 2 + at[3])

    def rows(first, size):
        return pl.ds(pl.multiple_of(first, TILE), size)

    number = {}
    for name in tasks:
        if tasks[name][1] is not None:
            number[name] = len(number)

    def arrives_with(name):
        if name[0] == "D":
            return ("D", name[1], name[2])
        if name[0] in ("YA", "YB"):
            return ("Y", name[1], name[2])
        if (name[0], name[-1]) in (("Z", NZ // 2), ("X", NX // 2)):
            return (name[0], name[1], name[2])
        return name

    together = {}
    for name in number:
        together.setdefault(arrives_with(name), []).append(name)
    slot = {key: i for i, key in enumerate(together)}
    groups = {}
    for name in number:
        key = (name[0][0],) if name[0][0] in "WB" else ({"Z": "Z", "X": "X", "D": "X"}.get(name[0], "Y"), name[1], name[2])
        groups.setdefault(key, len(groups))

    def group_of(name):
        key = (name[0][0],) if name[0][0] in "WB" else ({"Z": "Z", "X": "X", "D": "X"}.get(name[0], "Y"), name[1], name[2])
        return groups[key]

    def target(name, at):
        kind = name[0]
        if kind == "D":
            return moved(at, "k", 1)
        axis = {"Z": "z", "X": "x", "B": "z"}.get(kind, "y")
        return moved(at, axis, SIGN[name[1] if kind[0] in "WB" else name[3]])

    def source(name, at):
        kind = name[0]
        if kind == "D":
            return moved(at, "k", 1)
        axis = {"Z": "z", "X": "x", "B": "z"}.get(kind, "y")
        return moved(at, axis, -SIGN[name[1] if kind[0] in "WB" else name[3]])

    def span(first, half):
        if half is None:
            return rows(first, 2 * TILE)
        return rows(first + half * TILE, TILE)

    def ends(name, at):
        kind = name[0]
        if kind == "B":
            ref = bits.at[moved(at, "z", -SIGN[name[1]] * (name[2] - 1))[1]]
            return ref, ref
        if kind == "W1":
            d = name[1]
            return far_ref.at[moved(at, "y", SIGN[d])[0]], wr.at[0 if d == "-" else 1]
        if kind == "W2a":
            h = 0 if name[1] == "+" else 1
            return far_ref.at[moved(at, "y", 2)[0], pl.ds(h * TILE, TILE)], stage.at[h]
        if kind == "W2b":
            h = 0 if name[1] == "+" else 1
            return stage.at[h], wr.at[2, pl.ds(h * TILE, TILE)]
        p, c, d = name[1:4]
        if kind == "Z":
            s = name[4]
            first = moved(at, "z", -SIGN[d] * (s - 1))[1] * (2 * TILE)
            half = None if s < NZ // 2 else (0 if d == "+" else 1)
            ref = xz[p][c].at[span(first, half)]
            return ref, ref
        if kind in "XD":
            whole = xr[p][c] if p < 2 else lg[0][c]
            if kind == "X":
                s = name[4]
                from_x = moved(at, "x", -SIGN[d] * (s - 1))[2]
                half = None if s < NX // 2 else (0 if d == "+" else 1)
            else:
                by, half = {"0": 0, "+": -1, "-": 1, "f": 2}[d], None
                from_x = moved(at, "x", by)[2]
            ref = whole.at[span((from_x * 2 + at[3]) * (2 * TILE), half)]
            return ref, ref
        i = 0 if d == "+" else 1
        top, low = pl.ds(i * TILE, TILE), pl.ds((1 - i) * TILE, TILE)
        if kind == "Y1":
            return p2[p][c].at[top], y1[p][c].at[i]
        if kind == "YA":
            return ps[p][c].at[i, top], yr[p][c].at[i, top]
        return ps[p][c].at[i, low], yr[p][c].at[i, low]

    def descriptor(name, at, to):
        src, dst = ends(name, at)
        return pltpu.make_async_remote_copy(
            src_ref=src, dst_ref=dst, send_sem=send_sem.at[group_of(name)], recv_sem=recv_sem.at[slot[arrives_with(name)]],
            device_id=device(to), device_id_type=MESH)

    def arrival(name):
        key = arrives_with(name)
        if len(together[key]) == 1:
            dst = ends(name, source(name, me))[1]
        else:
            kind, p, c = key
            dst = xr[0][c].at[pl.ds(0, {"D": 8, "Y": 4, "Z": 2, "X": 2}[kind] * TILE)]
        return pltpu.make_async_remote_copy(
            src_ref=dst, dst_ref=dst, send_sem=send_sem.at[0], recv_sem=recv_sem.at[slot[key]],
            device_id=device(source(name, me)), device_id_type=MESH)

    own_z = rows(me[1] * (2 * TILE), 2 * TILE)
    own_r = rows(r * (2 * TILE), 2 * TILE)

    def loads(c):
        piece = block_hbm.at[:, pl.ds(offsets[c], widths[c])]
        return (pltpu.make_async_copy(piece, xz[0][c].at[own_z], load_sem.at[c, 0]),
                pltpu.make_async_copy(piece, xr[0][c].at[own_r], load_sem.at[c, 1]))

    def emit(c):
        cols = pl.ds(offsets[c], widths[c])
        return pltpu.make_async_copy(gram_ref.at[:, cols], gram_hbm.at[:, cols], out_sem.at[c, 1])

    def store(c):
        return pltpu.make_async_copy(lg[0][c].at[own_r], logs_hbm.at[:, pl.ds(offsets[c], widths[c])], out_sem.at[c, 0])

    for c in range(chunks):
        for copy in loads(c):
            copy.start()
    send_copy = pltpu.make_async_copy(send_hbm, send_ref, misc_sem.at[0])
    degree_copy = pltpu.make_async_copy(degree_hbm, degree_ref, misc_sem.at[1])
    for copy in (send_copy, degree_copy):
        copy.start()
    peers = [moved(me, axis, by) for axis in "zyx" for by in (1, -1)] + [moved(me, "k", 1)]
    barrier = pltpu.get_barrier_semaphore()
    for peer in peers:
        pl.semaphore_signal(barrier, inc=1, device_id=device(peer), device_id_type=MESH)
    send_copy.wait()
    bits[me[1]] = jnp.zeros(bits.shape[1:], bits.dtype)
    bits[me[1], pl.ds(0, 1), pl.ds(0, NY * NZ)] = send_ref[...]
    pl.semaphore_wait(barrier, len(peers))

    def dot(a, b):
        return jnp.dot(a, b, preferred_element_type=jnp.float32)

    def widen(j):
        slot = "0+-2".index(j)
        out = pl.ds("2+-0".index(j) * 2 * TILE, 2 * TILE)
        y = moved(me, "y", {"0": 0, "+": 1, "-": -1, "2": 2}[j])[0]
        for z in range(NZ):
            told = bits[z, pl.ds(0, 1), :].astype(jnp.float32)
            lane = lax.broadcasted_iota(jnp.int32, told.shape, 1)
            bit = jnp.sum(jnp.where(lane == y * NZ + me[1], told, 0.0), axis=1, keepdims=True)
            if j == "0":
                piece = far_ref[me[0], :, pl.ds(z * TILE, TILE)]
            else:
                piece = wr[slot - 1, :, pl.ds(z * TILE, TILE)]
            piece = piece.astype(jnp.float32)
            wide[out, pl.ds(z * 2 * TILE, TILE)] = (piece * (1.0 - bit)).astype(jnp.bfloat16)
            wide[out, pl.ds(z * 2 * TILE + TILE, TILE)] = (piece * bit).astype(jnp.bfloat16)

    def run(name):
        kind = name[0]
        if kind == "L":
            for copy in loads(name[1]):
                copy.wait()
        elif kind == "E":
            widen(name[1])
        elif kind == "H":
            degree_copy.wait()
            for h in range(2):
                degrees = degree_ref[pl.ds(h, 1), :].astype(jnp.float32)
                div_ref[pl.ds(h * TILE, TILE), :] = jnp.broadcast_to(degrees, (TILE, TILE)).T
        elif kind == "C":
            p, c, j = name[1:]
            if j == "0":
                acc[p][c][...] = dot(wide[pl.ds(6 * TILE, 2 * TILE), :], xz[p][c][...])
            elif j == "2":
                p2[p][c][...] = dot(wide[pl.ds(0, 2 * TILE), :], xz[p][c][...]).astype(jnp.bfloat16)
            else:
                made = dot(wide[pl.ds(2 * TILE, 4 * TILE), :], xz[p][c][...])
                for i in range(2):
                    part = made[2 * i * TILE:(2 + 2 * i) * TILE]
                    pf[p][c][i] = part[i * TILE:(i + 1) * TILE]
                    ps[p][c][i, pl.ds((1 - i) * TILE, TILE)] = part[(1 - i) * TILE:(2 - i) * TILE].astype(jnp.bfloat16)
        elif kind == "R":
            p, c = name[1:]
            acc[p][c][...] += dot(row_ref[...], xr[p][c][...])
        elif kind == "A":
            p, c, d = name[1:]
            i = 0 if d == "+" else 1
            ps[p][c][i, pl.ds(i * TILE, TILE)] = (pf[p][c][i] + y1[p][c][i].astype(jnp.float32)).astype(jnp.bfloat16)
        elif kind == "F":
            p, c = name[1:]
            summed = acc[p][c][...] + yr[p][c][0].astype(jnp.float32) + yr[p][c][1].astype(jnp.float32)
            divisor = jnp.concatenate([div_ref[...]] * (widths[c] // TILE), axis=1)
            power = (summed / divisor).astype(jnp.bfloat16)
            if p == 0:
                xz[1][c][own_z] = power
                xr[1][c][own_r] = power
            else:
                total = xr[1][c][own_r].astype(jnp.float32) + power.astype(jnp.float32)
                lg[0][c][own_r] = jnp.log(jnp.maximum(3.0 * total, 1.0)).astype(jnp.bfloat16)
                store(c).start()
        else:
            for c in range(chunks):
                first, count = offsets[c] // TILE, widths[c] // TILE

                @pl.when((r >= first) & (r < first + count))
                def _():
                    mine = pl.ds(pl.multiple_of((r - first) * TILE, TILE), TILE)
                    flip[...] = lg[0][c][:, mine].T

            for c in range(chunks):
                made = dot(flip[...], lg[0][c][...])
                gram_ref[:, pl.ds(offsets[c], widths[c])] = made * (1.0 / flip.shape[1])
                emit(c).start()

    waited = set()
    for name in order:
        for dep in tasks[name][0]:
            if dep[0] == "got" and dep[1] not in waited:
                waited.update(together[arrives_with(dep[1])])
                arrival(dep[1]).wait_recv()
        if name in number:
            descriptor(name, me, target(name, me)).start()
        else:
            run(name)
    for c in range(chunks):
        store(c).wait()
        emit(c).wait()
    for key, i in groups.items():
        if key[0] == "W":
            sent = far_ref
        elif key[0] == "B":
            sent = bits.at[pl.ds(0, NZ - 1)]
        else:
            kind, p, c = key
            sent = xz[0][c].at[pl.ds(0, (6 if kind == "Y" else 14) * TILE)]
        pltpu.make_async_remote_copy(
            src_ref=sent, dst_ref=sent, send_sem=send_sem.at[i], recv_sem=recv_sem.at[0],
            device_id=device(moved(me, "k", 1)), device_id_type=MESH).wait_send()


def body(block, degree, tile_values, tile_rows, tile_cols, tile_count, send_tiles):
    near, far = build_dense(tile_rows, tile_cols, tile_count, tile_values)
    rows_here, features = block.shape
    widths = WIDTHS
    tasks = task_list(widths)
    names = list(tasks)
    order = [names[i] for i in ORDER]
    hbm = pl.BlockSpec(memory_space=pl.ANY)
    vmem = pl.BlockSpec(memory_space=pltpu.VMEM)
    column, ranks = NZ * 2 * TILE, 2 * NX
    bf16, f32 = jnp.bfloat16, jnp.float32

    def kernel(*refs):
        step_kernel(tasks, order, widths, *refs)

    def each(lead, dtype):
        return [pltpu.VMEM((*lead, w), dtype) for w in widths]

    both = [
        each((column,), bf16), each((ranks * 2 * TILE,), bf16), each((2 * TILE,), bf16), each((2, 2 * TILE), bf16),
        each((2, TILE), f32), each((2, TILE), bf16), each((2, 2 * TILE), bf16), each((2 * TILE,), f32),
    ]
    return pl.pallas_call(
        kernel,
        out_shape=(
            jax.ShapeDtypeStruct((rows_here, features), bf16),
            jax.ShapeDtypeStruct((features // ranks, features), f32),
        ),
        in_specs=[hbm, vmem, vmem, hbm, hbm],
        out_specs=(hbm, hbm),
        scratch_shapes=[
            [[b, b] for b in both] + [[each((ranks * 2 * TILE,), bf16)]],
            pltpu.VMEM((4 * 2 * TILE, column), bf16),
            pltpu.VMEM((3, 2 * TILE, NZ * TILE), bf16),
            pltpu.VMEM((2, TILE, NZ * TILE), bf16),
            pltpu.VMEM((NZ, 8, TILE), jnp.int32),
            pltpu.VMEM((TILE, ranks * 2 * TILE), bf16),
            pltpu.VMEM((1, NY * NZ), jnp.int32),
            pltpu.VMEM((2, TILE), jnp.int32),
            pltpu.VMEM((2 * TILE, TILE), f32),
            pltpu.VMEM((features // ranks, features), f32),
            pltpu.SemaphoreType.DMA((len(widths), 2)),
            pltpu.SemaphoreType.DMA((2,)),
            pltpu.SemaphoreType.DMA((len(widths), 2)),
            pltpu.SemaphoreType.DMA((8 * len(widths) + 2,)),
            pltpu.SemaphoreType.DMA((14 * 2 * len(widths) + 4 * len(widths) + 13,)),
        ],
        compiler_params=pltpu.CompilerParams(
            collective_id=0, has_side_effects=True, vmem_limit_bytes=LIMIT),
    )(block, near, far, send_tiles, degree.reshape(2, TILE))


def solution(mesh):
    placed = (
        P(("grp", "row"), None),
        P(("grp", "row")),
        P(("grp", "row"), None, None),
        P(("grp", "row")),
        P(("grp", "row")),
        P(("grp", "row")),
        P(("grp", "row"), None),
    )
    return jax.shard_map(
        body,
        mesh=mesh,
        in_specs=placed,
        out_specs=(P(("grp", "row"), None), P(("grp", "row"), None)),
        check_vma=False,
    )
```

time: 139 us -> 123 us (0.88)
  Pallas kernels: 130 us -> 118 us
  local copies, waits for them, and re-layouts: 8.13 us -> 3.19 us
    pallas_call x1, Pallas kernels: 127 us -> 116 us  [body(): pl.pallas_call(kernel, out_shape=(jax.ShapeDtypeStruct((rows_here, featur...]
    unnamed x18 -> x10, local copies, waits for them, and re-layouts: 8.13 us -> 3.19 us
where the time goes in v2:
time: 123 us
  Pallas kernels  118 us (96%)
  local copies, waits for them, and re-layouts  3.19 us (3%)
  between operations  1.35 us (1%)
    pallas_call x1, Pallas kernels, body(): pl.pallas_call(kernel, out_shape=(jax.ShapeDtypeStruct((rows_here, featur...  116 us
    unnamed x10, local copies, waits for them, and re-layouts  3.19 us

profile of v2, /device:TPU:1, one launch (start us, length us, event | category | flops | bytes accessed | tf_op | source)
XLA Modules:
  0.0 123.2 jit_solution(17950590563533841841)
XLA Ops:
  0.6 0.0 copy-start.3
  0.6 0.0 copy-start.2
  1.3 0.7 multiply_add_fusion.cell_s
  2.0 0.0 copy-start
  2.0 1.6 %copy-done = bf16[64,128,128]{2,1,0:T(8,128)(2,1)S(1)} copy-done((bf16[64,128,128]{2,1,0:T(8,128)(2,1)S(1)}, bf16[64,128,128]{2,1,0:T(8,128)(2,1)}, u32[]{:S(2)}) %copy-start) | copy-done | bytes 2097176
  3.6 0.0 copy-start.1
  3.6 2.0 %shard_map.86 = (bf16[256,2048]{1,0:T(8,128)(2,1)S(1)}, bf16[4,256,1024]{2,1,0:T(8,128)(2,1)S(1)}) custom-call(s32[64]{0:T(128)S(1)} %multiply_add_fusion.cell_s, s32[1]{0:T(128)S(6)} %copy.11.count_s, bf16[64,128,128]{2,1,0:T(8,128)(2,1)S(1)} %copy-done), custom_call_target="tpu_custom_call" | custom-call | tf_op jit(solution)/shard_map/pallas_call | solution.py:66
  5.6 0.0 copy-done.3
  5.6 0.0 copy-done.2
  5.6 0.0 copy-done.1
  5.6 115.9 %shard_map.87 = (bf16[256,1024]{1,0:T(8,128)(2,1)S(1)}, f32[128,1024]{1,0:T(8,128)S(1)}) custom-call(bf16[256,1024]{1,0:T(8,128)(2,1)S(1)} %copy-done.1, bf16[256,2048]{1,0:T(8,128)(2,1)S(1)} %get-tuple-element.4.refs_1_, bf16[4,256,1024]{2,1,0:T(8,128)(2,1)S(1)} %get-tuple-element.5.refs_2_, s32[1,32]{1,0:T(1,128)S(1)} %copy-done.3, s32[2,128]{1,0:T(2,128)S(1)} %bitcast.1), custom_call_target="tpu_custom_call" | custom-call | tf_op jit(solution)/shard_map/pallas_call | solution.py:472
  121.6 0.8 copy.12
  122.4 0.8 copy.13
Async XLA Ops:
  0.6 5.0 %copy-start.3 = (s32[1,32]{1,0:T(1,128)S(1)}, s32[1,32]{1,0:T(1,128)}, u32[]{:S(2)}) copy-start(s32[1,32]{1,0:T(1,128)} %refs_3_.1) | copy-start | bytes 388
  0.6 5.0 %copy-start.2 = (s32[256]{0:T(256)S(1)}, s32[256]{0:T(256)}, u32[]{:S(2)}) copy-start(s32[256]{0:T(256)} %param.8) | copy-start | bytes 3076
  2.0 1.6 %copy-start = (bf16[64,128,128]{2,1,0:T(8,128)(2,1)S(1)}, bf16[64,128,128]{2,1,0:T(8,128)(2,1)}, u32[]{:S(2)}) copy-start(bf16[64,128,128]{2,1,0:T(8,128)(2,1)} %values.1) | copy-start | bytes 6291460
  3.6 2.1 %copy-start.1 = (bf16[256,1024]{1,0:T(8,128)(2,1)S(1)}, bf16[256,1024]{1,0:T(8,128)(2,1)}, u32[]{:S(2)}) copy-start(bf16[256,1024]{1,0:T(8,128)(2,1)} %refs_0_.1) | copy-start | bytes 1572868

commit v3 on v2

--- a/solution.py
+++ b/solution.py
@@ -16,19 +16,19 @@
 LATE = {"z": 2.3, "y": 2.8, "x": 5.0, "d": 4.0, "X": 2.5, "D": 1.5}
 MESH = pl.DeviceIdType.MESH
 ORDER = (
-    48, 53, 49, 8, 18, 19, 23, 78, 0, 108, 11, 4, 83, 50, 59, 121, 9, 27, 12, 1, 5, 24, 20, 113, 7, 61, 54, 13,
-    138, 87, 57, 139, 89, 2, 10, 79, 21, 25, 119, 29, 3, 143, 6, 93, 63, 55, 51, 120, 22, 26, 80, 149, 15, 91, 28, 84,
-    117, 31, 32, 90, 140, 30, 56, 144, 52, 16, 58, 17, 35, 62, 43, 147, 39, 109, 14, 36, 85, 81, 141, 44, 150, 40, 65, 73,
-    69, 88, 60, 41, 45, 122, 42, 114, 46, 110, 34, 66, 74, 153, 33, 70, 145, 37, 86, 71, 64, 82, 38, 75, 72, 76, 115, 142,
-    47, 111, 172, 92, 67, 146, 168, 176, 68, 118, 77, 205, 201, 152, 197, 148, 94, 95, 116, 96, 103, 104, 112, 124, 151, 99, 173, 207,
-    155, 100, 157, 169, 156, 163, 202, 177, 160, 198, 127, 105, 125, 106, 101, 129, 102, 126, 159, 174, 133, 170, 97, 98, 165, 203, 166, 199,
-    178, 180, 107, 164, 135, 130, 208, 206, 161, 131, 154, 226, 230, 234, 236, 162, 211, 171, 136, 132, 210, 158, 175, 167, 284, 288, 123, 134,
-    200, 292, 128, 204, 137, 231, 227, 184, 188, 240, 294, 192, 185, 259, 255, 293, 237, 179, 193, 189, 285, 213, 221, 181, 217, 289, 214, 232,
-    222, 228, 235, 194, 182, 265, 260, 190, 191, 298, 256, 212, 195, 183, 215, 219, 218, 223, 290, 238, 263, 295, 286, 224, 209, 220, 269, 186,
-    233, 229, 187, 196, 241, 261, 257, 216, 313, 266, 225, 291, 287, 315, 242, 250, 246, 243, 323, 258, 247, 262, 251, 321, 244, 239, 300, 308,
-    304, 301, 248, 249, 252, 253, 264, 271, 279, 316, 314, 275, 305, 325, 319, 299, 272, 310, 309, 267, 297, 324, 296, 322, 311, 306, 307, 276,
-    280, 268, 245, 254, 331, 329, 281, 282, 277, 278, 270, 326, 302, 273, 327, 303, 312, 320, 347, 345, 274, 333, 283, 339, 337, 330, 317, 318,
-    332, 348, 346, 340, 338, 334, 342, 341, 350, 336, 349, 351, 335, 343, 328, 352, 344, 353,
+    47, 52, 18, 19, 8, 23, 105, 27, 134, 31, 11, 76, 48, 12, 29, 4, 58, 56, 0, 77, 7, 53, 20, 9, 24, 57, 30, 1,
+    143, 28, 49, 145, 5, 135, 60, 54, 110, 59, 32, 6, 10, 25, 81, 114, 21, 85, 2, 87, 13, 50, 139, 34, 119, 3, 22, 26,
+    106, 33, 62, 63, 55, 146, 78, 111, 140, 51, 82, 15, 17, 35, 40, 43, 116, 90, 107, 16, 36, 144, 136, 41, 61, 14, 44, 112,
+    79, 141, 39, 42, 150, 45, 86, 64, 37, 88, 108, 72, 83, 137, 69, 38, 46, 167, 163, 66, 65, 80, 70, 73, 148, 115, 142, 84,
+    149, 117, 68, 74, 138, 109, 91, 113, 175, 71, 67, 171, 92, 164, 168, 93, 89, 101, 75, 195, 173, 191, 98, 151, 122, 118, 94, 99,
+    127, 130, 124, 165, 169, 159, 172, 176, 203, 120, 121, 147, 102, 156, 95, 97, 100, 123, 103, 196, 201, 192, 152, 131, 96, 199, 128, 126,
+    153, 170, 129, 166, 174, 177, 132, 155, 104, 223, 158, 219, 161, 197, 125, 193, 160, 227, 229, 133, 179, 247, 257, 205, 184, 157, 181, 154,
+    187, 251, 220, 178, 224, 255, 200, 180, 162, 202, 188, 198, 194, 287, 279, 275, 183, 233, 185, 189, 285, 248, 186, 252, 221, 225, 230, 207,
+    204, 212, 215, 260, 276, 228, 182, 190, 283, 305, 280, 258, 253, 286, 303, 209, 289, 249, 208, 211, 222, 234, 226, 214, 217, 256, 206, 216,
+    213, 232, 277, 259, 281, 210, 250, 254, 306, 288, 284, 235, 240, 243, 236, 218, 311, 278, 313, 244, 282, 241, 263, 271, 304, 268, 231, 264,
+    261, 239, 245, 242, 237, 291, 296, 269, 299, 292, 315, 290, 272, 267, 312, 273, 314, 270, 297, 262, 300, 238, 246, 319, 321, 295, 298, 301,
+    265, 309, 266, 274, 329, 327, 316, 293, 294, 302, 337, 335, 320, 323, 307, 322, 330, 328, 336, 338, 333, 325, 332, 310, 341, 340, 324, 317,
+    318, 339, 326, 308, 331, 334, 342, 343,
 )
 SIGN = {"+": 1, "-": -1}
 
@@ -106,7 +106,7 @@
         for c in range(chunks):
             rank = p * chunks + c
             part = widths[c] / sum(widths)
-            product = 2 * (2 * TILE) * (NZ * 2 * TILE) * max(widths[c], 192) / RATE
+            product = 2 * (2 * TILE) * (NZ * 2 * TILE) * max(widths[c], 190) / RATE
             own = [("L", c)] if p == 0 else [("F", p - 1, c)]
             if p == 0:
                 task(("L", c), [], None, 0, 0.05, rank)
@@ -137,11 +137,12 @@
             task(("C", p, c, "0"), column + [("E", "0")], None, 0, product * 0.95, rank)
             task(("R", p, c), row + [("C", p, c, "0"), ("H",)], None, 0, product * 1.2, rank)
             arrived = []
+            crossed = [got(("Y1", p, c, d)) for d in "+-"]
+            task(("A", p, c), crossed + [("C", p, c, "s")], None, 0, 0.1, rank)
             for d in "+-":
                 task(("Y1", p, c, d), [("C", p, c, "2")], "y" + d, part, 0.05, rank)
                 task(("YB", p, c, d), [("C", p, c, "s")], "y" + d, part, 0.05, rank)
-                task(("A", p, c, d), [got(("Y1", p, c, d)), ("C", p, c, "s")], None, 0, 0.05, rank)
-                task(("YA", p, c, d), [("A", p, c, d)], "y" + d, part, 0.05, rank)
+                task(("YA", p, c, d), [("A", p, c)], "y" + d, part, 0.05, rank)
                 arrived += [got(("YB", p, c, d)), got(("YA", p, c, d))]
             task(("F", p, c), arrived + [("R", p, c), ("H",)] + own, None, 0, 0.15, rank)
     task(("G",), gram_deps, None, 0, 0.95, 99)
@@ -186,9 +187,9 @@
     return order, now
 
 
-def step_kernel(tasks, order, widths, block_hbm, row_ref, far_ref, send_hbm, degree_hbm, logs_hbm, gram_hbm,
-                per_chunk, wide, wr, stage, bits, flip, send_ref, degree_ref, div_ref, gram_ref,
-                load_sem, misc_sem, out_sem, send_sem, recv_sem):
+def step_kernel(tasks, order, widths, block_hbm, row_ref, far_ref, send_hbm, degree_hbm, logs_ref, gram_ref,
+                per_chunk, wide, wr, stage, bits, flip, send_ref, degree_ref, div_ref,
+                load_sem, misc_sem, send_sem, recv_sem):
     chunks = len(widths)
     offsets = [sum(widths[:c]) for c in range(chunks)]
     xz, xr, p2, ps, pf, y1, yr, acc, lg = per_chunk
@@ -219,6 +220,8 @@
     def arrives_with(name):
         if name[0] == "D":
             return ("D", name[1], name[2])
+        if name[0] == "Y1":
+            return ("Y1", name[1], name[2])
         if name[0] in ("YA", "YB"):
             return ("Y", name[1], name[2])
         if (name[0], name[-1]) in (("Z", NZ // 2), ("X", NX // 2)):
@@ -231,11 +234,11 @@
     slot = {key: i for i, key in enumerate(together)}
     groups = {}
     for name in number:
-        key = (name[0][0],) if name[0][0] in "WB" else ({"Z": "Z", "X": "X", "D": "X"}.get(name[0], "Y"), name[1], name[2])
+        key = (name[0][0],) if name[0][0] in "WB" else ({"Z": "Z", "X": "X", "D": "X"}.get(name[0], "Y"), name[1])
         groups.setdefault(key, len(groups))
 
     def group_of(name):
-        key = (name[0][0],) if name[0][0] in "WB" else ({"Z": "Z", "X": "X", "D": "X"}.get(name[0], "Y"), name[1], name[2])
+        key = (name[0][0],) if name[0][0] in "WB" else ({"Z": "Z", "X": "X", "D": "X"}.get(name[0], "Y"), name[1])
         return groups[key]
 
     def target(name, at):
@@ -309,7 +312,7 @@
             dst = ends(name, source(name, me))[1]
         else:
             kind, p, c = key
-            dst = xr[0][c].at[pl.ds(0, {"D": 8, "Y": 4, "Z": 2, "X": 2}[kind] * TILE)]
+            dst = xr[0][c].at[pl.ds(0, {"D": 8, "Y": 4, "Y1": 2, "Z": 2, "X": 2}[kind] * TILE)]
         return pltpu.make_async_remote_copy(
             src_ref=dst, dst_ref=dst, send_sem=send_sem.at[0], recv_sem=recv_sem.at[slot[key]],
             device_id=device(source(name, me)), device_id_type=MESH)
@@ -321,13 +324,6 @@
         piece = block_hbm.at[:, pl.ds(offsets[c], widths[c])]
         return (pltpu.make_async_copy(piece, xz[0][c].at[own_z], load_sem.at[c, 0]),
                 pltpu.make_async_copy(piece, xr[0][c].at[own_r], load_sem.at[c, 1]))
-
-    def emit(c):
-        cols = pl.ds(offsets[c], widths[c])
-        return pltpu.make_async_copy(gram_ref.at[:, cols], gram_hbm.at[:, cols], out_sem.at[c, 1])
-
-    def store(c):
-        return pltpu.make_async_copy(lg[0][c].at[own_r], logs_hbm.at[:, pl.ds(offsets[c], widths[c])], out_sem.at[c, 0])
 
     for c in range(chunks):
         for copy in loads(c):
@@ -392,9 +388,9 @@
             p, c = name[1:]
             acc[p][c][...] += dot(row_ref[...], xr[p][c][...])
         elif kind == "A":
-            p, c, d = name[1:]
-            i = 0 if d == "+" else 1
-            ps[p][c][i, pl.ds(i * TILE, TILE)] = (pf[p][c][i] + y1[p][c][i].astype(jnp.float32)).astype(jnp.bfloat16)
+            p, c = name[1:]
+            for i in range(2):
+                ps[p][c][i, pl.ds(i * TILE, TILE)] = (pf[p][c][i] + y1[p][c][i].astype(jnp.float32)).astype(jnp.bfloat16)
         elif kind == "F":
             p, c = name[1:]
             summed = acc[p][c][...] + yr[p][c][0].astype(jnp.float32) + yr[p][c][1].astype(jnp.float32)
@@ -405,8 +401,9 @@
                 xr[1][c][own_r] = power
             else:
                 total = xr[1][c][own_r].astype(jnp.float32) + power.astype(jnp.float32)
-                lg[0][c][own_r] = jnp.log(jnp.maximum(3.0 * total, 1.0)).astype(jnp.bfloat16)
-                store(c).start()
+                logs = jnp.log(jnp.maximum(3.0 * total, 1.0)).astype(jnp.bfloat16)
+                lg[0][c][own_r] = logs
+                logs_ref[:, pl.ds(offsets[c], widths[c])] = logs
         else:
             for c in range(chunks):
                 first, count = offsets[c] // TILE, widths[c] // TILE
@@ -419,7 +416,6 @@
             for c in range(chunks):
                 made = dot(flip[...], lg[0][c][...])
                 gram_ref[:, pl.ds(offsets[c], widths[c])] = made * (1.0 / flip.shape[1])
-                emit(c).start()
 
     waited = set()
     for name in order:
@@ -431,17 +427,13 @@
             descriptor(name, me, target(name, me)).start()
         else:
             run(name)
-    for c in range(chunks):
-        store(c).wait()
-        emit(c).wait()
     for key, i in groups.items():
         if key[0] == "W":
             sent = far_ref
         elif key[0] == "B":
             sent = bits.at[pl.ds(0, NZ - 1)]
         else:
-            kind, p, c = key
-            sent = xz[0][c].at[pl.ds(0, (6 if kind == "Y" else 14) * TILE)]
+            sent = wide.at[pl.ds(0, (3 if key[0] == "Y" else 7) * TILE)]
         pltpu.make_async_remote_copy(
             src_ref=sent, dst_ref=sent, send_sem=send_sem.at[i], recv_sem=recv_sem.at[0],
             device_id=device(moved(me, "k", 1)), device_id_type=MESH).wait_send()
@@ -476,7 +468,7 @@
             jax.ShapeDtypeStruct((features // ranks, features), f32),
         ),
         in_specs=[hbm, vmem, vmem, hbm, hbm],
-        out_specs=(hbm, hbm),
+        out_specs=(vmem, vmem),
         scratch_shapes=[
             [[b, b] for b in both] + [[each((ranks * 2 * TILE,), bf16)]],
             pltpu.VMEM((4 * 2 * TILE, column), bf16),
@@ -487,12 +479,10 @@
             pltpu.VMEM((1, NY * NZ), jnp.int32),
             pltpu.VMEM((2, TILE), jnp.int32),
             pltpu.VMEM((2 * TILE, TILE), f32),
-            pltpu.VMEM((features // ranks, features), f32),
             pltpu.SemaphoreType.DMA((len(widths), 2)),
             pltpu.SemaphoreType.DMA((2,)),
-            pltpu.SemaphoreType.DMA((len(widths), 2)),
-            pltpu.SemaphoreType.DMA((8 * len(widths) + 2,)),
-            pltpu.SemaphoreType.DMA((14 * 2 * len(widths) + 4 * len(widths) + 13,)),
+            pltpu.SemaphoreType.DMA((9,)),
+            pltpu.SemaphoreType.DMA((13 * 2 * len(widths) + 4 * len(widths) + 13,)),
         ],
         compiler_params=pltpu.CompilerParams(
             collective_id=0, has_side_effects=True, vmem_limit_bytes=LIMIT),

time: 123 us -> 121 us (0.984)
  Pallas kernels: 118 us -> 116 us
    pallas_call x1, Pallas kernels: 116 us -> 114 us  [body(): pl.pallas_call(kernel, out_shape=(jax.ShapeDtypeStruct((rows_here, featur...]
where the time goes in v3:
time: 121 us
  Pallas kernels  116 us (96%)
  local copies, waits for them, and re-layouts  3.19 us (3%)
  between operations  1.35 us (1%)
    pallas_call x1, Pallas kernels, body(): pl.pallas_call(kernel, out_shape=(jax.ShapeDtypeStruct((rows_here, featur...  114 us
    unnamed x10, local copies, waits for them, and re-layouts  3.19 us

profile of v3, /device:TPU:1, one launch (start us, length us, event | category | flops | bytes accessed | tf_op | source)
XLA Modules:
  0.0 120.9 jit_solution(12552635940896996868)
XLA Ops:
  0.6 0.0 copy-start.3
  0.6 0.0 copy-start.2
  1.3 0.7 multiply_add_fusion.cell_s
  2.0 0.0 copy-start
  2.0 1.6 %copy-done = bf16[64,128,128]{2,1,0:T(8,128)(2,1)S(1)} copy-done((bf16[64,128,128]{2,1,0:T(8,128)(2,1)S(1)}, bf16[64,128,128]{2,1,0:T(8,128)(2,1)}, u32[]{:S(2)}) %copy-start) | copy-done | bytes 2097176
  3.6 0.0 copy-start.1
  3.6 1.9 %shard_map.86 = (bf16[256,2048]{1,0:T(8,128)(2,1)S(1)}, bf16[4,256,1024]{2,1,0:T(8,128)(2,1)S(1)}) custom-call(s32[64]{0:T(128)S(1)} %multiply_add_fusion.cell_s, s32[1]{0:T(128)S(6)} %copy.11.count_s, bf16[64,128,128]{2,1,0:T(8,128)(2,1)S(1)} %copy-done), custom_call_target="tpu_custom_call" | custom-call | tf_op jit(solution)/shard_map/pallas_call | solution.py:66
  5.5 0.0 copy-done.3
  5.5 0.0 copy-done.2
  5.5 0.0 copy-done.1
  5.5 113.8 %shard_map.87 = (bf16[256,1024]{1,0:T(8,128)(2,1)S(1)}, f32[128,1024]{1,0:T(8,128)S(1)}) custom-call(bf16[256,1024]{1,0:T(8,128)(2,1)S(1)} %copy-done.1, bf16[256,2048]{1,0:T(8,128)(2,1)S(1)} %get-tuple-element.4.refs_1_, bf16[4,256,1024]{2,1,0:T(8,128)(2,1)S(1)} %get-tuple-element.5.refs_2_, s32[1,32]{1,0:T(1,128)S(1)} %copy-done.3, s32[2,128]{1,0:T(2,128)S(1)} %bitcast.1), custom_call_target="tpu_custom_call" | custom-call | tf_op jit(solution)/shard_map/pallas_call | solution.py:464
  119.3 0.8 copy.12
  120.1 0.8 copy.13
Async XLA Ops:
  0.6 4.9 %copy-start.3 = (s32[1,32]{1,0:T(1,128)S(1)}, s32[1,32]{1,0:T(1,128)}, u32[]{:S(2)}) copy-start(s32[1,32]{1,0:T(1,128)} %refs_3_.1) | copy-start | bytes 388
  0.6 4.9 %copy-start.2 = (s32[256]{0:T(256)S(1)}, s32[256]{0:T(256)}, u32[]{:S(2)}) copy-start(s32[256]{0:T(256)} %param.8) | copy-start | bytes 3076
  2.0 1.6 %copy-start = (bf16[64,128,128]{2,1,0:T(8,128)(2,1)S(1)}, bf16[64,128,128]{2,1,0:T(8,128)(2,1)}, u32[]{:S(2)}) copy-start(bf16[64,128,128]{2,1,0:T(8,128)(2,1)} %values.1) | copy-start | bytes 6291460
  3.6 1.9 %copy-start.1 = (bf16[256,1024]{1,0:T(8,128)(2,1)S(1)}, bf16[256,1024]{1,0:T(8,128)(2,1)}, u32[]{:S(2)}) copy-start(bf16[256,1024]{1,0:T(8,128)(2,1)} %refs_0_.1) | copy-start | bytes 1572868

commit v4 on v3

--- a/solution.py
+++ b/solution.py
@@ -16,19 +16,19 @@
 LATE = {"z": 2.3, "y": 2.8, "x": 5.0, "d": 4.0, "X": 2.5, "D": 1.5}
 MESH = pl.DeviceIdType.MESH
 ORDER = (
-    47, 52, 18, 19, 8, 23, 105, 27, 134, 31, 11, 76, 48, 12, 29, 4, 58, 56, 0, 77, 7, 53, 20, 9, 24, 57, 30, 1,
-    143, 28, 49, 145, 5, 135, 60, 54, 110, 59, 32, 6, 10, 25, 81, 114, 21, 85, 2, 87, 13, 50, 139, 34, 119, 3, 22, 26,
-    106, 33, 62, 63, 55, 146, 78, 111, 140, 51, 82, 15, 17, 35, 40, 43, 116, 90, 107, 16, 36, 144, 136, 41, 61, 14, 44, 112,
-    79, 141, 39, 42, 150, 45, 86, 64, 37, 88, 108, 72, 83, 137, 69, 38, 46, 167, 163, 66, 65, 80, 70, 73, 148, 115, 142, 84,
-    149, 117, 68, 74, 138, 109, 91, 113, 175, 71, 67, 171, 92, 164, 168, 93, 89, 101, 75, 195, 173, 191, 98, 151, 122, 118, 94, 99,
-    127, 130, 124, 165, 169, 159, 172, 176, 203, 120, 121, 147, 102, 156, 95, 97, 100, 123, 103, 196, 201, 192, 152, 131, 96, 199, 128, 126,
-    153, 170, 129, 166, 174, 177, 132, 155, 104, 223, 158, 219, 161, 197, 125, 193, 160, 227, 229, 133, 179, 247, 257, 205, 184, 157, 181, 154,
-    187, 251, 220, 178, 224, 255, 200, 180, 162, 202, 188, 198, 194, 287, 279, 275, 183, 233, 185, 189, 285, 248, 186, 252, 221, 225, 230, 207,
-    204, 212, 215, 260, 276, 228, 182, 190, 283, 305, 280, 258, 253, 286, 303, 209, 289, 249, 208, 211, 222, 234, 226, 214, 217, 256, 206, 216,
-    213, 232, 277, 259, 281, 210, 250, 254, 306, 288, 284, 235, 240, 243, 236, 218, 311, 278, 313, 244, 282, 241, 263, 271, 304, 268, 231, 264,
-    261, 239, 245, 242, 237, 291, 296, 269, 299, 292, 315, 290, 272, 267, 312, 273, 314, 270, 297, 262, 300, 238, 246, 319, 321, 295, 298, 301,
-    265, 309, 266, 274, 329, 327, 316, 293, 294, 302, 337, 335, 320, 323, 307, 322, 330, 328, 336, 338, 333, 325, 332, 310, 341, 340, 324, 317,
-    318, 339, 326, 308, 331, 334, 342, 343,
+    18, 19, 23, 11, 27, 134, 4, 105, 0, 47, 52, 8, 60, 114, 48, 135, 1, 12, 110, 76, 20, 24, 5, 7, 58, 9, 31, 53,
+    143, 87, 147, 2, 29, 10, 49, 81, 106, 145, 85, 115, 56, 21, 6, 13, 25, 119, 86, 50, 116, 54, 30, 3, 77, 89, 118, 90,
+    57, 22, 26, 59, 14, 82, 146, 107, 51, 33, 28, 120, 15, 55, 144, 111, 16, 32, 88, 78, 117, 17, 35, 139, 43, 37, 36, 40,
+    83, 108, 64, 69, 136, 41, 72, 34, 112, 63, 79, 44, 65, 39, 140, 42, 45, 73, 38, 109, 92, 70, 62, 148, 84, 68, 71, 137,
+    74, 113, 141, 80, 66, 61, 46, 173, 167, 163, 67, 75, 191, 122, 195, 91, 93, 199, 101, 138, 201, 98, 127, 142, 94, 168, 124, 164,
+    99, 102, 123, 121, 196, 97, 100, 103, 192, 130, 175, 151, 171, 152, 156, 200, 131, 153, 165, 169, 204, 203, 95, 96, 104, 223, 150, 159,
+    149, 126, 174, 219, 197, 193, 172, 129, 154, 177, 166, 125, 229, 128, 227, 132, 155, 170, 158, 161, 202, 224, 157, 160, 220, 198, 133, 251,
+    194, 255, 247, 228, 162, 230, 180, 275, 205, 179, 279, 283, 285, 187, 184, 257, 206, 232, 221, 225, 188, 185, 207, 212, 215, 208, 248, 252,
+    233, 178, 234, 181, 176, 183, 186, 261, 260, 284, 189, 258, 213, 276, 216, 280, 209, 222, 226, 211, 286, 214, 217, 210, 249, 253, 256, 182,
+    190, 281, 287, 303, 277, 305, 235, 240, 243, 250, 254, 218, 313, 311, 236, 244, 241, 278, 282, 237, 262, 288, 263, 268, 271, 306, 304, 239,
+    242, 245, 264, 291, 299, 259, 296, 272, 231, 269, 314, 312, 292, 289, 297, 267, 270, 273, 300, 238, 246, 319, 321, 295, 301, 298, 265, 290,
+    266, 318, 309, 316, 310, 274, 327, 329, 293, 294, 302, 337, 335, 322, 325, 308, 307, 320, 330, 328, 336, 338, 340, 323, 339, 315, 317, 341,
+    332, 326, 333, 324, 331, 334, 342, 343,
 )
 SIGN = {"+": 1, "-": -1}
 

time: 121 us -> 120 us (level)
  no operation moved by 1% of the time
where the time goes in v4:
time: 120 us
  Pallas kernels  115 us (96%)
  local copies, waits for them, and re-layouts  3.19 us (3%)
  between operations  1.35 us (1%)
    pallas_call x1, Pallas kernels, body(): pl.pallas_call(kernel, out_shape=(jax.ShapeDtypeStruct((rows_here, featur...  113 us
    unnamed x10, local copies, waits for them, and re-layouts  3.19 us

profile of v4, /device:TPU:1, one launch (start us, length us, event | category | flops | bytes accessed | tf_op | source)
XLA Modules:
  0.0 120.0 jit_solution(14155624941051845422)
XLA Ops:
  0.6 0.0 copy-start.3
  0.6 0.0 copy-start.2
  1.3 0.7 multiply_add_fusion.cell_s
  2.0 0.0 copy-start
  2.0 1.6 %copy-done = bf16[64,128,128]{2,1,0:T(8,128)(2,1)S(1)} copy-done((bf16[64,128,128]{2,1,0:T(8,128)(2,1)S(1)}, bf16[64,128,128]{2,1,0:T(8,128)(2,1)}, u32[]{:S(2)}) %copy-start) | copy-done | bytes 2097176
  3.6 0.0 copy-start.1
  3.6 1.9 %shard_map.86 = (bf16[256,2048]{1,0:T(8,128)(2,1)S(1)}, bf16[4,256,1024]{2,1,0:T(8,128)(2,1)S(1)}) custom-call(s32[64]{0:T(128)S(1)} %multiply_add_fusion.cell_s, s32[1]{0:T(128)S(6)} %copy.11.count_s, bf16[64,128,128]{2,1,0:T(8,128)(2,1)S(1)} %copy-done), custom_call_target="tpu_custom_call" | custom-call | tf_op jit(solution)/shard_map/pallas_call | solution.py:66
  5.5 0.0 copy-done.3
  5.5 0.0 copy-done.2
  5.5 0.0 copy-done.1
  5.5 112.8 %shard_map.87 = (bf16[256,1024]{1,0:T(8,128)(2,1)S(1)}, f32[128,1024]{1,0:T(8,128)S(1)}) custom-call(bf16[256,1024]{1,0:T(8,128)(2,1)S(1)} %copy-done.1, bf16[256,2048]{1,0:T(8,128)(2,1)S(1)} %get-tuple-element.4.refs_1_, bf16[4,256,1024]{2,1,0:T(8,128)(2,1)S(1)} %get-tuple-element.5.refs_2_, s32[1,32]{1,0:T(1,128)S(1)} %copy-done.3, s32[2,128]{1,0:T(2,128)S(1)} %bitcast.1), custom_call_target="tpu_custom_call" | custom-call | tf_op jit(solution)/shard_map/pallas_call | solution.py:464
  118.4 0.8 copy.12
  119.2 0.8 copy.13
Async XLA Ops:
  0.6 4.9 %copy-start.3 = (s32[1,32]{1,0:T(1,128)S(1)}, s32[1,32]{1,0:T(1,128)}, u32[]{:S(2)}) copy-start(s32[1,32]{1,0:T(1,128)} %refs_3_.1) | copy-start | bytes 388
  0.6 4.9 %copy-start.2 = (s32[256]{0:T(256)S(1)}, s32[256]{0:T(256)}, u32[]{:S(2)}) copy-start(s32[256]{0:T(256)} %param.8) | copy-start | bytes 3076
  2.0 1.6 %copy-start = (bf16[64,128,128]{2,1,0:T(8,128)(2,1)S(1)}, bf16[64,128,128]{2,1,0:T(8,128)(2,1)}, u32[]{:S(2)}) copy-start(bf16[64,128,128]{2,1,0:T(8,128)(2,1)} %values.1) | copy-start | bytes 6291460
  3.6 1.9 %copy-start.1 = (bf16[256,1024]{1,0:T(8,128)(2,1)S(1)}, bf16[256,1024]{1,0:T(8,128)(2,1)}, u32[]{:S(2)}) copy-start(bf16[256,1024]{1,0:T(8,128)(2,1)} %refs_0_.1) | copy-start | bytes 1572868
